TPU v7x, 16 devices: a 4x2x1 block of a 4x4x8 slice. The times are simulated.
16 devices in a mesh: dp: 2 (over y, z), ctx: 8 (over x, core).
Axes of the slice: x: 4, y: 2, z: 1, core: 2. Of those that a mesh axis runs over, the one named last changes fastest.
The devices are a block of a 4x4x8 slice.
Arguments:
- x_chunk: bfloat16 [4096, 768], P(('dp', 'ctx')), parts along dimension 0
- cache_len: int32 [2], P('dp'), parts along dimension 0
- k_cache: bfloat16 [2, 32768, 12, 64], P(None, ('dp', 'ctx')), parts along dimension 1
- v_cache: bfloat16 [2, 32768, 12, 64], P(None, ('dp', 'ctx')), parts along dimension 1
- k_local: bfloat16 [2, 512, 12, 64], P(None, 'dp'), parts along dimension 1
- v_local: bfloat16 [2, 512, 12, 64], P(None, 'dp'), parts along dimension 1
- g_attn: bfloat16 [4, 768], replicated
- g_mlp: bfloat16 [4, 768], replicated
- w_q: bfloat16 [4, 768, 768], replicated
- w_k: bfloat16 [4, 768, 768], replicated
- w_v: bfloat16 [4, 768, 768], replicated
- w_o: bfloat16 [4, 768, 768], replicated
- w_gate: bfloat16 [4, 768, 3072], replicated
- w_up: bfloat16 [4, 768, 3072], replicated
- w_down: bfloat16 [4, 3072, 768], replicated
Outputs:
- output: bfloat16 [4096, 768], P(('dp', 'ctx')), parts along dimension 0
There are 2 independent parts. A program takes and returns all parts, laid end to end along the dimension named above; an argument that names none is the same for every part.
All inputs are finite; a program needn't handle non-finite values.
Results may differ from a plain program's by a relative error of at most 0.02.
Values are sent between devices in bfloat16 or wider.
A program may use at most 768 MiB of HBM per device.

v0:
```python
import functools

import jax
import jax.numpy as jnp
from jax import lax
from jax.experimental import pallas as pl
from jax.experimental.pallas import tpu as pltpu
from jax.sharding import PartitionSpec as P

NORM_EPS = 1e-6
WINDOW = 4
LOG2E = 1.4426950408889634
NEG = -1e38
MESH_ID = pl.DeviceIdType.MESH
ROWS = 256
CHUNK = 256
STATS = 8


def slot_of(step):
    unit = step // 2
    return unit + unit // 2 - 2 * (unit // 3), step % 2


def global_kernel(n_chips, pair, len_ref, qkv_ref, kc_ref, vc_ref, out_ref,
                  k_own, v_own, k_sib, v_sib, kn_sib, vn_sib, q_all, k_ext, scores, part, parts,
                  own_sem, sib_send, sib_recv, q_send, q_recv, o_send, o_recv):
    q_ref, k_ref, v_ref = qkv_ref.at[0], qkv_ref.at[1], qkv_ref.at[2]
    heads, head_dim, slots = k_own.shape
    n_slots = 2 * n_chips
    me = lax.axis_index('ctx')
    chip, core = me // 2, me % 2
    first_head = heads * core
    other_head = heads * (1 - core)
    sibling = {'ctx': 2 * chip + (1 - core)}
    n_new = 2 * ROWS
    n_keys = 2 * slots + n_new

    barrier = pltpu.get_barrier_semaphore()
    for step in range(1, n_slots):
        pl.semaphore_signal(barrier, inc=1, device_id={'ctx': (me + step) % n_slots}, device_id_type=MESH_ID)

    def own_copies(head):
        return (pltpu.make_async_copy(kc_ref.at[pair, first_head + head], k_own.at[head], own_sem.at[0, head]),
                pltpu.make_async_copy(vc_ref.at[pair, first_head + head], v_own.at[head], own_sem.at[1, head]))

    def sib_copies(head):
        pairs = ((kc_ref.at[pair, other_head + head], k_sib.at[head]),
                 (vc_ref.at[pair, other_head + head], v_sib.at[head]),
                 (k_ref.at[other_head + head], kn_sib.at[head]),
                 (v_ref.at[other_head + head], vn_sib.at[head]))
        return [pltpu.make_async_remote_copy(src_ref=src, dst_ref=dst, send_sem=sib_send.at[which, head],
                                             recv_sem=sib_recv.at[which, head], device_id=sibling, device_id_type=MESH_ID)
                for which, (src, dst) in enumerate(pairs)]

    def target(dist, flip):
        return {'ctx': 2 * ((chip + dist) % n_chips) + (core + flip) % 2}

    def q_copy(dist, flip, head):
        slot = 2 * dist + flip
        their_head = heads * ((core + flip) % 2) + head
        return pltpu.make_async_remote_copy(src_ref=q_ref.at[their_head], dst_ref=q_all.at[slot, head],
                                            send_sem=q_send.at[slot, head], recv_sem=q_recv.at[slot, head],
                                            device_id=target(dist, flip), device_id_type=MESH_ID)

    def o_copy(dist, flip, head):
        slot = 2 * dist + flip
        owner = {'ctx': 2 * ((chip + n_chips - dist) % n_chips) + (core + flip) % 2}
        return pltpu.make_async_remote_copy(src_ref=part.at[slot, head], dst_ref=parts.at[slot, head],
                                            send_sem=o_send.at[slot, head], recv_sem=o_recv.at[slot, head],
                                            device_id=owner, device_id_type=MESH_ID)

    def start_own(head, carry):
        for copy in own_copies(head):
            copy.start()
        q_all[0, head] = q_ref[first_head + head]
        return carry

    lax.fori_loop(0, heads, start_own, 0)
    pl.semaphore_wait(barrier, n_slots - 1)

    def start_head(head, carry):
        for copy in sib_copies(head):
            copy.start()

        def start_q(step, inner):
            dist, flip = slot_of(step)
            q_copy(dist, flip, head).start()
            return inner

        lax.fori_loop(1, n_slots, start_q, 0)
        return carry

    lax.fori_loop(0, heads, start_head, 0)

    valid = len_ref[0]

    def prepare(head):
        for copy in own_copies(head):
            copy.wait()
        for copy in sib_copies(head):
            copy.wait_recv()
        width = 512
        row = lax.broadcasted_iota(jnp.int32, (head_dim, width), 0)
        col = lax.broadcasted_iota(jnp.int32, (head_dim, width), 1)
        for begin in range(0, n_keys, width):
            if begin < 2 * slots:
                source = k_own if begin < slots else k_sib
                at = begin % slots
                tile = source[head, :, at:at + width]
                device = me if begin < slots else 2 * chip + (1 - core)
                bias = jnp.where((row == 0) & (device * slots + at + col >= valid), NEG, 0.0)
            else:
                tile = jnp.concatenate([k_ref[first_head + head], kn_sib[head]], axis=1)
                bias = jnp.where((row == 1) & (col < ROWS) | (row == 2) & (col >= ROWS), 1.0, 0.0)
            buf = head % 2
            k_ext[buf, begin:begin + width, 0:2 * head_dim] = jnp.concatenate([tile, tile], axis=0).T
            k_ext[buf, begin:begin + width, 2 * head_dim:] = jnp.concatenate([tile, bias.astype(jnp.bfloat16)], axis=0).T

    def query_columns(head, dist, flip):
        slot = 2 * dist + flip
        full = q_all[slot, head].astype(jnp.float32) * (LOG2E * head_dim ** -0.5)
        high = full.astype(jnp.bfloat16)
        rest = full - high.astype(jnp.float32)
        middle = rest.astype(jnp.bfloat16)
        low = (rest - middle.astype(jnp.float32)).astype(jnp.bfloat16)
        q_dev = 2 * ((chip + n_chips - dist) % n_chips) + (core + flip) % 2
        row = lax.broadcasted_iota(jnp.int32, (head_dim, ROWS), 0)
        hide_own = jnp.where(q_dev < me, NEG, 0.0)
        hide_sib = jnp.where(q_dev < 2 * chip + (1 - core), NEG, 0.0)
        mask = jnp.where(row == 0, 1.0, jnp.where(row == 1, hide_own, jnp.where(row == 2, hide_sib, 0.0)))
        return jnp.concatenate([high, middle, low, mask.astype(jnp.bfloat16)], axis=0), q_dev

    def score_chunk(buf, columns, q_dev, begin, top):
        keys = pl.ds(begin, CHUNK)
        block = jnp.dot(k_ext[buf, keys, :], columns, preferred_element_type=jnp.float32)
        if begin >= 2 * slots:
            device = me if begin < 2 * slots + ROWS else 2 * chip + (1 - core)
            ahead = lax.broadcasted_iota(jnp.int32, (CHUNK, ROWS), 0) - lax.broadcasted_iota(jnp.int32, (CHUNK, ROWS), 1)
            block = jnp.where(ahead <= jnp.where(q_dev == device, 0, ROWS), block, NEG)
        scores[keys, :] = block
        return jnp.maximum(top, jnp.max(block.reshape(CHUNK // 8, 8, ROWS), axis=0))

    def value_chunk(head, base, begin, total, weighted):
        keys = pl.ds(begin, CHUNK)
        probs = jnp.exp2(scores[keys, :] - base)
        total = total + jnp.sum(probs.reshape(CHUNK // 8, 8, ROWS), axis=0)
        if begin < slots:
            values = v_own[head, :, begin:begin + CHUNK]
        elif begin < 2 * slots:
            values = v_sib[head, :, begin - slots:begin - slots + CHUNK]
        elif begin < 2 * slots + ROWS:
            values = v_ref[first_head + head]
        else:
            values = vn_sib[head]
        return total, weighted + jnp.dot(values, probs.astype(jnp.bfloat16), preferred_element_type=jnp.float32)

    no_top = jnp.full((8, ROWS), NEG, jnp.float32)

    prepare(0)
    columns, q_dev = query_columns(0, 0, 0)
    top = no_top
    for begin in range(0, n_keys, CHUNK):
        top = score_chunk(0, columns, q_dev, begin, top)

    def one_head(head, top):
        next_head = jnp.minimum(head + 1, heads - 1)

        @pl.when(head < heads - 1)
        def _():
            prepare(next_head)

        def one_step(step, top):
            dist, flip = slot_of(step)
            slot = 2 * dist + flip
            after = (step + 1) % n_slots
            dist_n, flip_n = slot_of(after)
            head_n = jnp.where(step == n_slots - 1, next_head, head)

            @pl.when(after > 0)
            def _():
                q_copy(dist_n, flip_n, head).wait_recv()

            columns, q_dev = query_columns(head_n, dist_n, flip_n)
            base = jnp.max(top, axis=0, keepdims=True)
            total = jnp.zeros((8, ROWS), jnp.float32)
            weighted = jnp.zeros((head_dim, ROWS), jnp.float32)
            new_top = no_top
            for begin in range(0, n_keys, CHUNK):
                total, weighted = value_chunk(head, base, begin, total, weighted)
                new_top = score_chunk(head_n % 2, columns, q_dev, begin, new_top)
            row = lax.broadcasted_iota(jnp.int32, (STATS, ROWS), 0)
            total = jnp.sum(total, axis=0, keepdims=True)
            part[slot, head, 0:head_dim, :] = weighted
            part[slot, head, head_dim:, :] = jnp.where(row == 0, base, total)

            @pl.when(step > 0)
            def _():
                o_copy(dist, flip, head).start()

            return new_top

        return lax.fori_loop(0, n_slots, one_step, top)

    lax.fori_loop(0, heads, one_head, top)

    def merge(head, carry):
        for flip in range(2):
            found = []
            for dist in range(n_chips):
                slot = 2 * dist + flip
                if slot == 0:
                    found.append((part[0, head, 0:head_dim, :], part[0, head, head_dim:head_dim + 1, :],
                                  part[0, head, head_dim + 1:head_dim + 2, :]))
                else:
                    o_copy(dist, flip, head).wait_recv()
                    found.append((parts[slot, head, 0:head_dim, :], parts[slot, head, head_dim:head_dim + 1, :],
                                  parts[slot, head, head_dim + 1:head_dim + 2, :]))
            peak = functools.reduce(jnp.maximum, [base for _, base, _ in found])
            scaled = [(weighted, total, jnp.exp2(base - peak)) for weighted, base, total in found]
            upper = sum(weighted * factor for weighted, _, factor in scaled)
            lower = sum(total * factor for _, total, factor in scaled)
            out_ref[heads * ((core + flip) % 2) + head] = (upper / lower).astype(jnp.bfloat16)
        return carry

    lax.fori_loop(0, heads, merge, 0)

    def finish(head, carry):
        for copy in sib_copies(head):
            copy.wait_send()

        def finish_step(step, inner):
            dist, flip = slot_of(step)
            q_copy(dist, flip, head).wait_send()
            o_copy(dist, flip, head).wait_send()
            return inner

        lax.fori_loop(1, n_slots, finish_step, 0)
        return carry

    lax.fori_loop(0, heads, finish, 0)


def global_attention(pair, n_dev, valid_len, qkv, cache_k, cache_v):
    _, all_heads, head_dim, rows = qkv.shape
    heads = all_heads // 2
    slots = cache_k.shape[-1]
    n_keys = 2 * (slots + rows)
    vmem = pl.BlockSpec(memory_space=pltpu.VMEM)
    bf16, f32 = jnp.bfloat16, jnp.float32
    return pl.pallas_call(
        functools.partial(global_kernel, n_dev // 2, pair),
        out_shape=jax.ShapeDtypeStruct((all_heads, head_dim, rows), bf16),
        in_specs=[pl.BlockSpec(memory_space=pltpu.SMEM), vmem,
                  pl.BlockSpec(memory_space=pl.ANY), pl.BlockSpec(memory_space=pl.ANY)],
        out_specs=vmem,
        scratch_shapes=[
            pltpu.VMEM((heads, head_dim, slots), bf16), pltpu.VMEM((heads, head_dim, slots), bf16),
            pltpu.VMEM((heads, head_dim, slots), bf16), pltpu.VMEM((heads, head_dim, slots), bf16),
            pltpu.VMEM((heads, head_dim, rows), bf16), pltpu.VMEM((heads, head_dim, rows), bf16),
            pltpu.VMEM((n_dev, heads, head_dim, rows), bf16),
            pltpu.VMEM((2, n_keys, 4 * head_dim), bf16),
            pltpu.VMEM((n_keys, rows), f32),
            pltpu.VMEM((n_dev, heads, head_dim + STATS, rows), f32),
            pltpu.VMEM((n_dev, heads, head_dim + STATS, rows), f32),
            pltpu.SemaphoreType.DMA((2, heads)),
            pltpu.SemaphoreType.DMA((4, heads)), pltpu.SemaphoreType.DMA((4, heads)),
            pltpu.SemaphoreType.DMA((n_dev, heads)), pltpu.SemaphoreType.DMA((n_dev, heads)),
            pltpu.SemaphoreType.DMA((n_dev, heads)), pltpu.SemaphoreType.DMA((n_dev, heads)),
        ],
        compiler_params=pltpu.CompilerParams(collective_id=pair, has_side_effects=True, vmem_limit_bytes=56 * 2 ** 20),
        name='global_attn_%d' % pair,
    )(valid_len, qkv, cache_k, cache_v)


def rms_rows(rows_in, gain_row):
    rows_f32 = rows_in.astype(jnp.float32)
    inv_rms = lax.rsqrt(jnp.mean(rows_f32 * rows_f32, axis=-1, keepdims=True) + NORM_EPS)
    return (rows_f32 * inv_rms * gain_row.astype(jnp.float32)).astype(jnp.bfloat16)


def mat(rows_in, weight):
    return jnp.dot(rows_in, weight, preferred_element_type=jnp.float32)


def dense_kernel(finish_layer, local_layer, n_dev, *refs):
    refs = list(refs)
    take = lambda count: [refs.pop(0) for _ in range(count)]
    x_ref, ga_ref, gm_ref = take(3)
    o_ref = take(1)[0] if finish_layer is not None else None
    wq, wk, wv, wo, wg, wu, wd = take(7)
    kl_ref, vl_ref = take(2) if local_layer is not None else (None, None)
    y_ref = take(1)[0]
    qkv_ref = take(1)[0] if local_layer is not None else None
    blocks, block_sem, rows_ref, acts, sums = take(5)
    n_rows, width = x_ref.shape
    n_ff = wg.shape[2] // width

    def weight_copy(source, at):
        return pltpu.make_async_copy(source, blocks.at[at], block_sem.at[at])

    def ff_copies(layer, base, part):
        span = pl.ds(pl.multiple_of(part * width, width), width)
        return [weight_copy(source, base + 3 * part + which)
                for which, source in enumerate((wg.at[layer, :, span], wu.at[layer, :, span], wd.at[layer, span, :]))]

    finish_base = 1
    local_base = (0 if finish_layer is None else 1 + 3 * n_ff) + 4
    next_base = local_base + 3 * n_ff
    plan = []
    if finish_layer is not None:
        plan += [weight_copy(wo.at[finish_layer], 0)]
        plan += [copy for part in range(n_ff) for copy in ff_copies(finish_layer, finish_base, part)]
    if local_layer is not None:
        plan += [weight_copy(w.at[local_layer], local_base - 4 + which) for which, w in enumerate((wk, wv, wq, wo))]
        plan += [copy for part in range(n_ff) for copy in ff_copies(local_layer, local_base, part)]
        plan += [weight_copy(w.at[local_layer + 1], next_base + which) for which, w in enumerate((wq, wk, wv))]
    started = [0]

    def fetch(limit):
        for copy in plan[started[0]:limit]:
            copy.start()
        started[0] = max(started[0], min(limit, len(plan)))

    fetch(WINDOW)
    if local_layer is not None:
        x_send, x_halo, klt, vlt, keys, values, queries, attn_t, local_sem, halo_send, halo_recv = take(11)
        me = lax.axis_index('ctx')
        barrier = pltpu.get_barrier_semaphore()
        after, before = (me + 1) % n_dev, (me + n_dev - 1) % n_dev
        for neighbour in (after, before):
            pl.semaphore_signal(barrier, inc=1, device_id={'ctx': neighbour}, device_id_type=MESH_ID)
        pair = local_layer // 2
        local_copies = [pltpu.make_async_copy(kl_ref.at[pair], klt, local_sem.at[0]), pltpu.make_async_copy(vl_ref.at[pair], vlt, local_sem.at[1])]
        halo = pltpu.make_async_remote_copy(src_ref=x_ref if finish_layer is None else x_send, dst_ref=x_halo, send_sem=halo_send,
                                            recv_sem=halo_recv, device_id={'ctx': after}, device_id_type=MESH_ID)
        for copy in local_copies:
            copy.start()
        if finish_layer is None:
            pl.semaphore_wait(barrier, 2)
            halo.start()

    def block(at):
        fetch(at + WINDOW)
        plan[at].wait()
        return blocks[at]

    def mlp(hidden, layer, base):
        fetch(base + 3 * n_ff)
        rows_ref[...] = rms_rows(hidden, gm_ref[layer:layer + 1, :])
        sums[...] = hidden.astype(jnp.float32)

        def activate(part):
            gate_pre = mat(rows_ref[...], blocks[base + 3 * part])
            up_pre = mat(rows_ref[...], blocks[base + 3 * part + 1])
            acts[part % 2] = (jax.nn.gelu(gate_pre, approximate=True) * up_pre).astype(jnp.bfloat16)

        def shrink(part):
            sums[...] += mat(acts[part % 2], blocks[base + 3 * part + 2])

        def arrive(part):
            for copy in ff_copies(layer, base, part):
                copy.wait()

        arrive(0)
        activate(0)

        def step(part, carry):
            arrive(part)
            shrink(part - 1)
            activate(part)
            return carry

        lax.fori_loop(1, n_ff, step, 0)
        fetch(base + 3 * n_ff + WINDOW)
        shrink(n_ff - 1)
        return sums[...].astype(jnp.bfloat16)

    hidden = x_ref[...]
    if finish_layer is not None:
        attn = o_ref[...].T
        hidden = (hidden.astype(jnp.float32) + mat(attn, block(0))).astype(jnp.bfloat16)
        hidden = mlp(hidden, finish_layer, finish_base)
    if local_layer is None:
        y_ref[...] = hidden
        return
    if finish_layer is not None:
        x_send[...] = hidden
        pl.semaphore_wait(barrier, 2)
        halo.start()

    heads, head_dim = kl_ref.shape[1], kl_ref.shape[2]
    at = local_base - 4
    gain = ga_ref[local_layer:local_layer + 1, :]
    rows_ref[...] = rms_rows(hidden, gain)
    key_block = block(at)
    keys[n_rows:, :] = mat(rows_ref[...], key_block).astype(jnp.bfloat16)
    value_block = block(at + 1)
    values[:, n_rows:] = mat(rows_ref[...], value_block).astype(jnp.bfloat16).T
    queries[...] = mat(rows_ref[...], block(at + 2)).astype(jnp.bfloat16).T
    for copy in local_copies:
        copy.wait()
    fetch(at + 4 + WINDOW)
    first = me == 0
    halo.wait_recv()
    rows_ref[...] = rms_rows(x_halo[...], gain)
    keys[:n_rows, :] = jnp.where(first, klt[...].reshape(width, n_rows).T, mat(rows_ref[...], blocks[at]).astype(jnp.bfloat16))
    values[:, :n_rows] = jnp.where(first, vlt[...].reshape(width, n_rows), mat(rows_ref[...], blocks[at + 1]).astype(jnp.bfloat16).T)
    ahead = lax.broadcasted_iota(jnp.int32, (2 * n_rows, n_rows), 0) - lax.broadcasted_iota(jnp.int32, (2 * n_rows, n_rows), 1)
    seen = (ahead > 0) & (ahead <= n_rows)
    row = lax.broadcasted_iota(jnp.int32, (2 * head_dim, n_rows), 0)

    def head_pair(pair_at, carry):
        lanes = pl.ds(pl.multiple_of(2 * head_dim * pair_at, 2 * head_dim), 2 * head_dim)
        for half in range(2):
            columns = jnp.where(row // head_dim == half, queries[lanes, :], 0.0).astype(jnp.bfloat16)
            block_scores = mat(keys[:, lanes], columns) * (LOG2E * head_dim ** -0.5)
            block_scores = jnp.where(seen, block_scores, NEG)
            probs = jnp.exp2(block_scores - jnp.max(block_scores, axis=0, keepdims=True))
            below = jnp.sum(probs, axis=0, keepdims=True)
            rows = pl.ds(pl.multiple_of(2 * head_dim * pair_at + half * head_dim, head_dim), head_dim)
            attn_t[rows, :] = (mat(values[rows, :], probs.astype(jnp.bfloat16)) / below).astype(jnp.bfloat16)
        return carry

    lax.fori_loop(0, heads // 2, head_pair, 0)
    hidden = (hidden.astype(jnp.float32) + mat(attn_t[...].T, block(at + 3))).astype(jnp.bfloat16)
    hidden = mlp(hidden, local_layer, local_base)
    y_ref[...] = hidden
    rows_ref[...] = rms_rows(hidden, ga_ref[local_layer + 1:local_layer + 2, :])
    fetch(len(plan))

    def project(which, carry):
        weight_copy(wq.at[local_layer + 1], next_base + which).wait()
        qkv_ref[which] = mat(rows_ref[...], blocks[next_base + which]).astype(jnp.bfloat16).T.reshape(qkv_ref.shape[1:])
        return carry

    lax.fori_loop(0, 3, project, 0)
    halo.wait_send()


def dense(finish_layer, local_layer, n_dev, x_rows, gains, attn_t, weights, local_t):
    n_rows, width = x_rows.shape
    n_ff = weights[4].shape[2] // width
    vmem = pl.BlockSpec(memory_space=pltpu.VMEM)
    hbm = pl.BlockSpec(memory_space=pl.ANY)
    bf16 = jnp.bfloat16
    n_blocks = (0 if finish_layer is None else 1 + 3 * n_ff) + (0 if local_layer is None else 7 + 3 * n_ff)
    args, in_specs = [x_rows, *gains], [vmem] * 3
    out_shape, out_specs = [jax.ShapeDtypeStruct(x_rows.shape, bf16)], [vmem]
    scratch = [pltpu.VMEM((n_blocks, width, width), bf16), pltpu.SemaphoreType.DMA((n_blocks,)),
               pltpu.VMEM(x_rows.shape, bf16), pltpu.VMEM((2, *x_rows.shape), bf16), pltpu.VMEM(x_rows.shape, jnp.float32)]
    if finish_layer is not None:
        args.append(attn_t)
        in_specs.append(vmem)
    args += weights
    in_specs += [hbm] * len(weights)
    params = {}
    if local_layer is not None:
        args += local_t
        in_specs += [hbm] * 2
        _, heads, head_dim, window = local_t[0].shape
        out_shape += [jax.ShapeDtypeStruct((3, heads, head_dim, n_rows), bf16)]
        out_specs += [vmem]
        scratch += [pltpu.VMEM(x_rows.shape, bf16), pltpu.VMEM(x_rows.shape, bf16),
                    pltpu.VMEM((heads, head_dim, window), bf16), pltpu.VMEM((heads, head_dim, window), bf16),
                    pltpu.VMEM((window + n_rows, width), bf16), pltpu.VMEM((width, window + n_rows), bf16),
                    pltpu.VMEM((width, n_rows), bf16), pltpu.VMEM((width, n_rows), bf16),
                    pltpu.SemaphoreType.DMA((2,)), pltpu.SemaphoreType.DMA, pltpu.SemaphoreType.DMA]
        params = dict(collective_id=8 + local_layer, has_side_effects=True)
    return pl.pallas_call(
        functools.partial(dense_kernel, finish_layer, local_layer, n_dev),
        out_shape=tuple(out_shape), in_specs=in_specs, out_specs=tuple(out_specs), scratch_shapes=scratch,
        compiler_params=pltpu.CompilerParams(vmem_limit_bytes=60 * 2 ** 20, **params),
        name='dense_%s_%s' % (finish_layer, local_layer),
    )(*args)


def solution(mesh):
    ctx_size = mesh.shape['ctx']
    row_spec = P(('dp', 'ctx'), None)
    cache_spec = P(None, ('dp', 'ctx'), None, None)
    local_spec = P(None, 'dp', None, None)
    in_specs = (row_spec, P('dp'), cache_spec, cache_spec, local_spec, local_spec) + (P(),) * 9

    def device_step(x_rows, cache_len, k_cache, v_cache, k_local, v_local, g_attn, g_mlp, *weights):
        by_slot = lambda array: jnp.transpose(array, (0, 2, 3, 1))
        cache_t = [by_slot(k_cache), by_slot(v_cache)]
        local_t = [by_slot(k_local), by_slot(v_local)]
        gains = [g_attn, g_mlp]
        hidden, finish_layer, attn_t = x_rows, None, None
        for pair in range(k_cache.shape[0]):
            hidden, qkv = dense(finish_layer, 2 * pair, ctx_size, hidden, gains, attn_t, weights, local_t)
            attn_t = global_attention(pair, ctx_size, cache_len, qkv, *cache_t)
            attn_t = attn_t.reshape(-1, attn_t.shape[-1])
            finish_layer = 2 * pair + 1
        return dense(finish_layer, None, ctx_size, hidden, gains, attn_t, weights, local_t)[0]

    return jax.shard_map(device_step, mesh=mesh, in_specs=in_specs, out_specs=row_spec, check_vma=False)
```

profile of v0, /device:TPU:113, one launch (start us, length us, event | category | flops | bytes accessed | tf_op | source)
XLA Modules:
  0.0 226.2 jit_solution(9758070169352669138)
XLA Ops:
  0.7 22.0 %dense_None_0.1 = (bf16[256,768]{1,0:T(8,128)(2,1)}, bf16[3,12,64,256]{3,2,1,0:T(8,128)(2,1)}) custom-call(bf16[256,768]{1,0:T(8,128)(2,1)} %refs_0_.1, bf16[4,768]{1,0:T(4,128)(2,1)} %refs_1_.5, bf16[4,768]{1,0:T(4,128)(2,1)} %refs_2_.5, bf16[4,768,768]{2,1,0:T(8,128)(2,1)} %refs_4_.5, bf16[4,768,768]{2,1,0:T(8,128)(2,1)} %refs_5_.5, ...), custom_call_target="tpu_custom_call" | custom-call | tf_op jit(solution)/shard_map/dense_None_0/pallas_call | solution.py:470
  22.7 83.6 %global_attn_0.1 = bf16[12,64,256]{2,1,0:T(8,128)(2,1)} custom-call(s32[1]{0:T(128)S(6)} %copy.16.len_ref, bf16[3,12,64,256]{3,2,1,0:T(8,128)(2,1)} %get-tuple-element.10.qkv_ref, bf16[2,12,64,2048]{3,2,1,0:T(8,128)(2,1)} %bitcast.6, bf16[2,12,64,2048]{3,2,1,0:T(8,128)(2,1)} %bitcast.8), custom_call_target="tpu_custom_call" | custom-call | tf_op jit(solution)/shard_map/global_attn_0/pallas_call | solution.py:251
  106.3 27.1 %dense_1_2.1 = (bf16[256,768]{1,0:T(8,128)(2,1)}, bf16[3,12,64,256]{3,2,1,0:T(8,128)(2,1)}) custom-call(bf16[256,768]{1,0:T(8,128)(2,1)} %get-tuple-element.9.refs_0_, bf16[4,768]{1,0:T(4,128)(2,1)} %refs_1_.5, bf16[4,768]{1,0:T(4,128)(2,1)} %refs_2_.5, bf16[768,256]{1,0:T(8,128)(2,1)} %bitcast.14, bf16[4,768,768]{2,1,0:T(8,128)(2,1)} %refs_4_.5, ...), custom_call_target="tpu_custom_call" | custom-call | tf_op jit(solution)/shard_map/dense_1_2/pallas_call | solution.py:470
  133.4 83.1 %global_attn_1.1 = bf16[12,64,256]{2,1,0:T(8,128)(2,1)} custom-call(s32[1]{0:T(128)S(6)} %copy.16.len_ref, bf16[3,12,64,256]{3,2,1,0:T(8,128)(2,1)} %get-tuple-element.12.qkv_ref, bf16[2,12,64,2048]{3,2,1,0:T(8,128)(2,1)} %bitcast.7, bf16[2,12,64,2048]{3,2,1,0:T(8,128)(2,1)} %bitcast.9), custom_call_target="tpu_custom_call" | custom-call | tf_op jit(solution)/shard_map/global_attn_1/pallas_call | solution.py:251
  216.5 9.5 %dense_3_None.1 = bf16[256,768]{1,0:T(8,128)(2,1)} custom-call(bf16[256,768]{1,0:T(8,128)(2,1)} %get-tuple-element.11.refs_0_, bf16[4,768]{1,0:T(4,128)(2,1)} %refs_1_.5, bf16[4,768]{1,0:T(4,128)(2,1)} %refs_2_.5, bf16[768,256]{1,0:T(8,128)(2,1)} %bitcast.15, bf16[4,768,768]{2,1,0:T(8,128)(2,1)} %refs_4_.5, bf16[4,768,768]{2,1,0:T(8,128)(2,1)} %refs_5_.5, ...), custom_call_target="tpu_custom_call" | custom-call | tf_op jit(solution)/shard_map/dense_3_None/pallas_call | solution.py:470
where the time goes:
time: 226 us
  Pallas kernels  225 us (100%)
    pallas_call x2, Pallas kernels, global_attention(): pl.pallas_call(functools.partial(global_kernel, n_dev // 2, pair), out_sh...  167 us
    pallas_call x3, Pallas kernels, dense(): pl.pallas_call(functools.partial(dense_kernel, finish_layer, local_layer,...  58.6 us

commit v1 on v0

--- a/solution.py
+++ b/solution.py
@@ -13,17 +13,19 @@
 NEG = -1e38
 MESH_ID = pl.DeviceIdType.MESH
 ROWS = 256
-CHUNK = 256
+SCORE_KEYS = 1152
+VALUE_KEYS = 128
 STATS = 8
 
 
-def slot_of(step):
-    unit = step // 2
-    return unit + unit // 2 - 2 * (unit // 3), step % 2
+def slot_of(step, head, n_slots):
+    place = jnp.where(head == 0, step, n_slots - 1 - step)
+    unit = place // 2
+    return unit + unit // 2 - 2 * (unit // 3), place % 2
 
 
 def global_kernel(n_chips, pair, len_ref, qkv_ref, kc_ref, vc_ref, out_ref,
-                  k_own, v_own, k_sib, v_sib, kn_sib, vn_sib, q_all, k_ext, scores, part, parts,
+                  k_own, v_own, k_sib, v_sib, kn_sib, vn_sib, q_all, k_twice, k_mask, scores, part, parts,
                   own_sem, sib_send, sib_recv, q_send, q_recv, o_send, o_recv):
     q_ref, k_ref, v_ref = qkv_ref.at[0], qkv_ref.at[1], qkv_ref.at[2]
     heads, head_dim, slots = k_own.shape
@@ -84,7 +86,7 @@
             copy.start()
 
         def start_q(step, inner):
-            dist, flip = slot_of(step)
+            dist, flip = slot_of(step, 0, n_slots)
             q_copy(dist, flip, head).start()
             return inner
 
@@ -114,8 +116,8 @@
                 tile = jnp.concatenate([k_ref[first_head + head], kn_sib[head]], axis=1)
                 bias = jnp.where((row == 1) & (col < ROWS) | (row == 2) & (col >= ROWS), 1.0, 0.0)
             buf = head % 2
-            k_ext[buf, begin:begin + width, 0:2 * head_dim] = jnp.concatenate([tile, tile], axis=0).T
-            k_ext[buf, begin:begin + width, 2 * head_dim:] = jnp.concatenate([tile, bias.astype(jnp.bfloat16)], axis=0).T
+            k_twice[buf, begin:begin + width, :] = jnp.concatenate([tile, tile], axis=0).T
+            k_mask[buf, begin:begin + width, :] = jnp.concatenate([tile, bias.astype(jnp.bfloat16)], axis=0).T
 
     def query_columns(head, dist, flip):
         slot = 2 * dist + flip
@@ -132,35 +134,43 @@
         return jnp.concatenate([high, middle, low, mask.astype(jnp.bfloat16)], axis=0), q_dev
 
     def score_chunk(buf, columns, q_dev, begin, top):
-        keys = pl.ds(begin, CHUNK)
-        block = jnp.dot(k_ext[buf, keys, :], columns, preferred_element_type=jnp.float32)
-        if begin >= 2 * slots:
-            device = me if begin < 2 * slots + ROWS else 2 * chip + (1 - core)
-            ahead = lax.broadcasted_iota(jnp.int32, (CHUNK, ROWS), 0) - lax.broadcasted_iota(jnp.int32, (CHUNK, ROWS), 1)
-            block = jnp.where(ahead <= jnp.where(q_dev == device, 0, ROWS), block, NEG)
-        scores[keys, :] = block
-        return jnp.maximum(top, jnp.max(block.reshape(CHUNK // 8, 8, ROWS), axis=0))
+        keys = pl.ds(begin, SCORE_KEYS)
+        rows = jnp.concatenate([k_twice[buf, keys, :], k_mask[buf, keys, :]], axis=1)
+        block = jnp.dot(rows, columns, preferred_element_type=jnp.float32)
+        plain = min(max(2 * slots - begin, 0), SCORE_KEYS)
+        pieces = [block[:plain]] if plain else []
+        for at in range(plain, SCORE_KEYS, ROWS):
+            device = me if begin + at < 2 * slots + ROWS else 2 * chip + (1 - core)
+            ahead = lax.broadcasted_iota(jnp.int32, (ROWS, ROWS), 0) - lax.broadcasted_iota(jnp.int32, (ROWS, ROWS), 1)
+            pieces.append(jnp.where(ahead <= jnp.where(q_dev == device, 0, ROWS), block[at:at + ROWS], NEG))
+        at = begin
+        for piece in pieces:
+            scores[pl.ds(at, piece.shape[0]), :] = piece
+            top = jnp.maximum(top, jnp.max(piece.reshape(piece.shape[0] // 8, 8, ROWS), axis=0))
+            at += piece.shape[0]
+        return top
 
     def value_chunk(head, base, begin, total, weighted):
-        keys = pl.ds(begin, CHUNK)
-        probs = jnp.exp2(scores[keys, :] - base)
-        total = total + jnp.sum(probs.reshape(CHUNK // 8, 8, ROWS), axis=0)
+        probs = jnp.exp2(scores[pl.ds(begin, VALUE_KEYS), :] - base)
+        total = total + jnp.sum(probs.reshape(VALUE_KEYS // 8, 8, ROWS), axis=0)
         if begin < slots:
-            values = v_own[head, :, begin:begin + CHUNK]
+            values = v_own[head, :, begin:begin + VALUE_KEYS]
         elif begin < 2 * slots:
-            values = v_sib[head, :, begin - slots:begin - slots + CHUNK]
+            values = v_sib[head, :, begin - slots:begin - slots + VALUE_KEYS]
         elif begin < 2 * slots + ROWS:
-            values = v_ref[first_head + head]
+            values = v_ref[first_head + head, :, begin - 2 * slots:begin - 2 * slots + VALUE_KEYS]
         else:
-            values = vn_sib[head]
+            values = vn_sib[head, :, begin - 2 * slots - ROWS:begin - 2 * slots - ROWS + VALUE_KEYS]
         return total, weighted + jnp.dot(values, probs.astype(jnp.bfloat16), preferred_element_type=jnp.float32)
 
+    order = sorted([(begin + VALUE_KEYS, 0, begin) for begin in range(0, n_keys, VALUE_KEYS)]
+                   + [(begin + SCORE_KEYS, 1, begin) for begin in range(0, n_keys, SCORE_KEYS)])
     no_top = jnp.full((8, ROWS), NEG, jnp.float32)
 
     prepare(0)
     columns, q_dev = query_columns(0, 0, 0)
     top = no_top
-    for begin in range(0, n_keys, CHUNK):
+    for begin in range(0, n_keys, SCORE_KEYS):
         top = score_chunk(0, columns, q_dev, begin, top)
 
     def one_head(head, top):
@@ -171,30 +181,33 @@
             prepare(next_head)
 
         def one_step(step, top):
-            dist, flip = slot_of(step)
+            dist, flip = slot_of(step, head, n_slots)
             slot = 2 * dist + flip
             after = (step + 1) % n_slots
-            dist_n, flip_n = slot_of(after)
             head_n = jnp.where(step == n_slots - 1, next_head, head)
-
-            @pl.when(after > 0)
+            dist_n, flip_n = slot_of(after, head_n, n_slots)
+            remote_n = (2 * dist_n + flip_n > 0) & ((step < n_slots - 1) | (head < heads - 1))
+
+            @pl.when(remote_n)
             def _():
-                q_copy(dist_n, flip_n, head).wait_recv()
+                q_copy(dist_n, flip_n, head_n).wait_recv()
 
             columns, q_dev = query_columns(head_n, dist_n, flip_n)
             base = jnp.max(top, axis=0, keepdims=True)
             total = jnp.zeros((8, ROWS), jnp.float32)
             weighted = jnp.zeros((head_dim, ROWS), jnp.float32)
             new_top = no_top
-            for begin in range(0, n_keys, CHUNK):
-                total, weighted = value_chunk(head, base, begin, total, weighted)
-                new_top = score_chunk(head_n % 2, columns, q_dev, begin, new_top)
+            for _, kind, begin in order:
+                if kind == 0:
+                    total, weighted = value_chunk(head, base, begin, total, weighted)
+                else:
+                    new_top = score_chunk(head_n % 2, columns, q_dev, begin, new_top)
             row = lax.broadcasted_iota(jnp.int32, (STATS, ROWS), 0)
             total = jnp.sum(total, axis=0, keepdims=True)
             part[slot, head, 0:head_dim, :] = weighted
             part[slot, head, head_dim:, :] = jnp.where(row == 0, base, total)
 
-            @pl.when(step > 0)
+            @pl.when(slot > 0)
             def _():
                 o_copy(dist, flip, head).start()
 
@@ -230,7 +243,7 @@
             copy.wait_send()
 
         def finish_step(step, inner):
-            dist, flip = slot_of(step)
+            dist, flip = slot_of(step, 0, n_slots)
             q_copy(dist, flip, head).wait_send()
             o_copy(dist, flip, head).wait_send()
             return inner
@@ -259,7 +272,7 @@
             pltpu.VMEM((heads, head_dim, slots), bf16), pltpu.VMEM((heads, head_dim, slots), bf16),
             pltpu.VMEM((heads, head_dim, rows), bf16), pltpu.VMEM((heads, head_dim, rows), bf16),
             pltpu.VMEM((n_dev, heads, head_dim, rows), bf16),
-            pltpu.VMEM((2, n_keys, 4 * head_dim), bf16),
+            pltpu.VMEM((2, n_keys, 2 * head_dim), bf16), pltpu.VMEM((2, n_keys, 2 * head_dim), bf16),
             pltpu.VMEM((n_keys, rows), f32),
             pltpu.VMEM((n_dev, heads, head_dim + STATS, rows), f32),
             pltpu.VMEM((n_dev, heads, head_dim + STATS, rows), f32),

time: 226 us -> 214 us (0.947)
  Pallas kernels: 225 us -> 213 us
    pallas_call x2, Pallas kernels: 167 us -> 155 us  [global_attention(): pl.pallas_call(functools.partial(global_kernel, n_dev // 2, pair), out_sh...]
where the time goes in v1:
time: 214 us
  Pallas kernels  213 us (100%)
    pallas_call x2, Pallas kernels, global_attention(): pl.pallas_call(functools.partial(global_kernel, n_dev // 2, pair), out_sh...  155 us
    pallas_call x3, Pallas kernels, dense(): pl.pallas_call(functools.partial(dense_kernel, finish_layer, local_layer,...  58.2 us

profile of v1, /device:TPU:113, one launch (start us, length us, event | category | flops | bytes accessed | tf_op | source)
XLA Modules:
  0.0 213.6 jit_solution(9559895045321412804)
XLA Ops:
  0.7 21.9 %dense_None_0.1 = (bf16[256,768]{1,0:T(8,128)(2,1)}, bf16[3,12,64,256]{3,2,1,0:T(8,128)(2,1)}) custom-call(bf16[256,768]{1,0:T(8,128)(2,1)} %refs_0_.1, bf16[4,768]{1,0:T(4,128)(2,1)} %refs_1_.5, bf16[4,768]{1,0:T(4,128)(2,1)} %refs_2_.5, bf16[4,768,768]{2,1,0:T(8,128)(2,1)} %refs_4_.5, bf16[4,768,768]{2,1,0:T(8,128)(2,1)} %refs_5_.5, ...), custom_call_target="tpu_custom_call" | custom-call | tf_op jit(solution)/shard_map/dense_None_0/pallas_call | solution.py:483
  22.5 76.8 %global_attn_0.1 = bf16[12,64,256]{2,1,0:T(8,128)(2,1)} custom-call(s32[1]{0:T(128)S(6)} %copy.16.len_ref, bf16[3,12,64,256]{3,2,1,0:T(8,128)(2,1)} %get-tuple-element.10.qkv_ref, bf16[2,12,64,2048]{3,2,1,0:T(8,128)(2,1)} %bitcast.6, bf16[2,12,64,2048]{3,2,1,0:T(8,128)(2,1)} %bitcast.8), custom_call_target="tpu_custom_call" | custom-call | tf_op jit(solution)/shard_map/global_attn_0/pallas_call | solution.py:264
  99.3 26.9 %dense_1_2.1 = (bf16[256,768]{1,0:T(8,128)(2,1)}, bf16[3,12,64,256]{3,2,1,0:T(8,128)(2,1)}) custom-call(bf16[256,768]{1,0:T(8,128)(2,1)} %get-tuple-element.9.refs_0_, bf16[4,768]{1,0:T(4,128)(2,1)} %refs_1_.5, bf16[4,768]{1,0:T(4,128)(2,1)} %refs_2_.5, bf16[768,256]{1,0:T(8,128)(2,1)} %bitcast.14, bf16[4,768,768]{2,1,0:T(8,128)(2,1)} %refs_4_.5, ...), custom_call_target="tpu_custom_call" | custom-call | tf_op jit(solution)/shard_map/dense_1_2/pallas_call | solution.py:483
  126.2 77.7 %global_attn_1.1 = bf16[12,64,256]{2,1,0:T(8,128)(2,1)} custom-call(s32[1]{0:T(128)S(6)} %copy.16.len_ref, bf16[3,12,64,256]{3,2,1,0:T(8,128)(2,1)} %get-tuple-element.12.qkv_ref, bf16[2,12,64,2048]{3,2,1,0:T(8,128)(2,1)} %bitcast.7, bf16[2,12,64,2048]{3,2,1,0:T(8,128)(2,1)} %bitcast.9), custom_call_target="tpu_custom_call" | custom-call | tf_op jit(solution)/shard_map/global_attn_1/pallas_call | solution.py:264
  203.9 9.5 %dense_3_None.1 = bf16[256,768]{1,0:T(8,128)(2,1)} custom-call(bf16[256,768]{1,0:T(8,128)(2,1)} %get-tuple-element.11.refs_0_, bf16[4,768]{1,0:T(4,128)(2,1)} %refs_1_.5, bf16[4,768]{1,0:T(4,128)(2,1)} %refs_2_.5, bf16[768,256]{1,0:T(8,128)(2,1)} %bitcast.15, bf16[4,768,768]{2,1,0:T(8,128)(2,1)} %refs_4_.5, bf16[4,768,768]{2,1,0:T(8,128)(2,1)} %refs_5_.5, ...), custom_call_target="tpu_custom_call" | custom-call | tf_op jit(solution)/shard_map/dense_3_None/pallas_call | solution.py:483

commit v2 on v1

--- a/solution.py
+++ b/solution.py
@@ -18,14 +18,59 @@
 STATS = 8
 
 
+def rms_rows(rows_in, gain_row):
+    rows_f32 = rows_in.astype(jnp.float32)
+    inv_rms = lax.rsqrt(jnp.mean(rows_f32 * rows_f32, axis=-1, keepdims=True) + NORM_EPS)
+    return (rows_f32 * inv_rms * gain_row.astype(jnp.float32)).astype(jnp.bfloat16)
+
+
+def mat(rows_in, weight):
+    return jnp.dot(rows_in, weight, preferred_element_type=jnp.float32)
+
+
+def ff_copies(weights, blocks, block_sem, layer, base, part):
+    wg, wu, wd = weights
+    width = wd.shape[2]
+    span = pl.ds(pl.multiple_of(part * width, width), width)
+    return [pltpu.make_async_copy(source, blocks.at[base + 3 * part + which], block_sem.at[base + 3 * part + which])
+            for which, source in enumerate((wg.at[layer, :, span], wu.at[layer, :, span], wd.at[layer, span, :]))]
+
+
+def mlp_rows(hidden, gain, n_ff, blocks, base, arrive, rows_ref, acts, sums):
+    rows_ref[...] = rms_rows(hidden, gain)
+    sums[...] = hidden.astype(jnp.float32)
+
+    def activate(part):
+        gate_pre = mat(rows_ref[...], blocks[base + 3 * part])
+        up_pre = mat(rows_ref[...], blocks[base + 3 * part + 1])
+        acts[part % 2] = (jax.nn.gelu(gate_pre, approximate=True) * up_pre).astype(jnp.bfloat16)
+
+    def shrink(part):
+        sums[...] += mat(acts[part % 2], blocks[base + 3 * part + 2])
+
+    arrive(0)
+    activate(0)
+
+    def step(part, carry):
+        arrive(part)
+        shrink(part - 1)
+        activate(part)
+        return carry
+
+    lax.fori_loop(1, n_ff, step, 0)
+    shrink(n_ff - 1)
+    return sums[...].astype(jnp.bfloat16)
+
+
 def slot_of(step, head, n_slots):
     place = jnp.where(head == 0, step, n_slots - 1 - step)
     unit = place // 2
     return unit + unit // 2 - 2 * (unit // 3), place % 2
 
 
-def global_kernel(n_chips, pair, len_ref, qkv_ref, kc_ref, vc_ref, out_ref,
+def global_kernel(n_chips, pair, len_ref, qkv_ref, x_ref, gm_ref, wo, wg, wu, wd, kc_ref, vc_ref, y_ref,
                   k_own, v_own, k_sib, v_sib, kn_sib, vn_sib, q_all, k_twice, k_mask, scores, part, parts,
+                  blocks, block_sem, rows_ref, acts, sums, attn_t,
                   own_sem, sib_send, sib_recv, q_send, q_recv, o_send, o_recv):
     q_ref, k_ref, v_ref = qkv_ref.at[0], qkv_ref.at[1], qkv_ref.at[2]
     heads, head_dim, slots = k_own.shape
@@ -94,6 +139,14 @@
         return carry
 
     lax.fori_loop(0, heads, start_head, 0)
+
+    layer = 2 * pair + 1
+    n_rows, width = x_ref.shape
+    n_ff = wg.shape[2] // width
+    out_copy = pltpu.make_async_copy(wo.at[layer], blocks.at[0], block_sem.at[0])
+
+    def mlp_copies(part):
+        return ff_copies((wg, wu, wd), blocks, block_sem, layer, 1, part)
 
     valid = len_ref[0]
 
@@ -168,6 +221,10 @@
     no_top = jnp.full((8, ROWS), NEG, jnp.float32)
 
     prepare(0)
+    out_copy.start()
+    for part_at in range(n_ff):
+        for copy in mlp_copies(part_at):
+            copy.start()
     columns, q_dev = query_columns(0, 0, 0)
     top = no_top
     for begin in range(0, n_keys, SCORE_KEYS):
@@ -233,10 +290,19 @@
             scaled = [(weighted, total, jnp.exp2(base - peak)) for weighted, base, total in found]
             upper = sum(weighted * factor for weighted, _, factor in scaled)
             lower = sum(total * factor for _, total, factor in scaled)
-            out_ref[heads * ((core + flip) % 2) + head] = (upper / lower).astype(jnp.bfloat16)
+            attn_t[heads * ((core + flip) % 2) + head] = (upper / lower).astype(jnp.bfloat16)
         return carry
 
     lax.fori_loop(0, heads, merge, 0)
+    out_copy.wait()
+    attn = attn_t[...].reshape(width, n_rows).T
+    hidden = (x_ref[...].astype(jnp.float32) + mat(attn, blocks[0])).astype(jnp.bfloat16)
+
+    def arrive(part_at):
+        for copy in mlp_copies(part_at):
+            copy.wait()
+
+    y_ref[...] = mlp_rows(hidden, gm_ref[layer:layer + 1, :], n_ff, blocks, 1, arrive, rows_ref, acts, sums)
 
     def finish(head, carry):
         for copy in sib_copies(head):
@@ -254,18 +320,19 @@
     lax.fori_loop(0, heads, finish, 0)
 
 
-def global_attention(pair, n_dev, valid_len, qkv, cache_k, cache_v):
+def global_layer(pair, n_dev, valid_len, qkv, x_rows, mlp_gain, weights, cache_k, cache_v):
     _, all_heads, head_dim, rows = qkv.shape
     heads = all_heads // 2
     slots = cache_k.shape[-1]
     n_keys = 2 * (slots + rows)
+    width = x_rows.shape[1]
+    n_blocks = 1 + 3 * (weights[1].shape[2] // width)
     vmem = pl.BlockSpec(memory_space=pltpu.VMEM)
     bf16, f32 = jnp.bfloat16, jnp.float32
     return pl.pallas_call(
         functools.partial(global_kernel, n_dev // 2, pair),
-        out_shape=jax.ShapeDtypeStruct((all_heads, head_dim, rows), bf16),
-        in_specs=[pl.BlockSpec(memory_space=pltpu.SMEM), vmem,
-                  pl.BlockSpec(memory_space=pl.ANY), pl.BlockSpec(memory_space=pl.ANY)],
+        out_shape=jax.ShapeDtypeStruct(x_rows.shape, bf16),
+        in_specs=[pl.BlockSpec(memory_space=pltpu.SMEM), vmem, vmem, vmem] + [pl.BlockSpec(memory_space=pl.ANY)] * 6,
         out_specs=vmem,
         scratch_shapes=[
             pltpu.VMEM((heads, head_dim, slots), bf16), pltpu.VMEM((heads, head_dim, slots), bf16),
@@ -276,58 +343,35 @@
             pltpu.VMEM((n_keys, rows), f32),
             pltpu.VMEM((n_dev, heads, head_dim + STATS, rows), f32),
             pltpu.VMEM((n_dev, heads, head_dim + STATS, rows), f32),
+            pltpu.VMEM((n_blocks, width, width), bf16), pltpu.SemaphoreType.DMA((n_blocks,)),
+            pltpu.VMEM(x_rows.shape, bf16), pltpu.VMEM((2, *x_rows.shape), bf16), pltpu.VMEM(x_rows.shape, f32),
+            pltpu.VMEM((all_heads, head_dim, rows), bf16),
             pltpu.SemaphoreType.DMA((2, heads)),
             pltpu.SemaphoreType.DMA((4, heads)), pltpu.SemaphoreType.DMA((4, heads)),
             pltpu.SemaphoreType.DMA((n_dev, heads)), pltpu.SemaphoreType.DMA((n_dev, heads)),
             pltpu.SemaphoreType.DMA((n_dev, heads)), pltpu.SemaphoreType.DMA((n_dev, heads)),
         ],
-        compiler_params=pltpu.CompilerParams(collective_id=pair, has_side_effects=True, vmem_limit_bytes=56 * 2 ** 20),
-        name='global_attn_%d' % pair,
-    )(valid_len, qkv, cache_k, cache_v)
-
-
-def rms_rows(rows_in, gain_row):
-    rows_f32 = rows_in.astype(jnp.float32)
-    inv_rms = lax.rsqrt(jnp.mean(rows_f32 * rows_f32, axis=-1, keepdims=True) + NORM_EPS)
-    return (rows_f32 * inv_rms * gain_row.astype(jnp.float32)).astype(jnp.bfloat16)
-
-
-def mat(rows_in, weight):
-    return jnp.dot(rows_in, weight, preferred_element_type=jnp.float32)
-
-
-def dense_kernel(finish_layer, local_layer, n_dev, *refs):
-    refs = list(refs)
-    take = lambda count: [refs.pop(0) for _ in range(count)]
-    x_ref, ga_ref, gm_ref = take(3)
-    o_ref = take(1)[0] if finish_layer is not None else None
-    wq, wk, wv, wo, wg, wu, wd = take(7)
-    kl_ref, vl_ref = take(2) if local_layer is not None else (None, None)
-    y_ref = take(1)[0]
-    qkv_ref = take(1)[0] if local_layer is not None else None
-    blocks, block_sem, rows_ref, acts, sums = take(5)
+        compiler_params=pltpu.CompilerParams(collective_id=pair, has_side_effects=True, vmem_limit_bytes=60 * 2 ** 20),
+        name='global_%d' % pair,
+    )(valid_len, qkv, x_rows, mlp_gain, *weights, cache_k, cache_v)
+
+
+def local_kernel(layer, n_dev, x_ref, ga_ref, gm_ref, wq, wk, wv, wo, wg, wu, wd, kl_ref, vl_ref, y_ref, qkv_ref,
+                 blocks, block_sem, rows_ref, acts, sums, x_halo, klt, vlt, keys, values, queries, attn_t,
+                 local_sem, halo_send, halo_recv):
     n_rows, width = x_ref.shape
     n_ff = wg.shape[2] // width
+    base, next_base = 4, 4 + 3 * n_ff
 
     def weight_copy(source, at):
         return pltpu.make_async_copy(source, blocks.at[at], block_sem.at[at])
 
-    def ff_copies(layer, base, part):
-        span = pl.ds(pl.multiple_of(part * width, width), width)
-        return [weight_copy(source, base + 3 * part + which)
-                for which, source in enumerate((wg.at[layer, :, span], wu.at[layer, :, span], wd.at[layer, span, :]))]
-
-    finish_base = 1
-    local_base = (0 if finish_layer is None else 1 + 3 * n_ff) + 4
-    next_base = local_base + 3 * n_ff
-    plan = []
-    if finish_layer is not None:
-        plan += [weight_copy(wo.at[finish_layer], 0)]
-        plan += [copy for part in range(n_ff) for copy in ff_copies(finish_layer, finish_base, part)]
-    if local_layer is not None:
-        plan += [weight_copy(w.at[local_layer], local_base - 4 + which) for which, w in enumerate((wk, wv, wq, wo))]
-        plan += [copy for part in range(n_ff) for copy in ff_copies(local_layer, local_base, part)]
-        plan += [weight_copy(w.at[local_layer + 1], next_base + which) for which, w in enumerate((wq, wk, wv))]
+    def mlp_copies(part):
+        return ff_copies((wg, wu, wd), blocks, block_sem, layer, base, part)
+
+    plan = [weight_copy(w.at[layer], which) for which, w in enumerate((wk, wv, wq, wo))]
+    plan += [copy for part in range(n_ff) for copy in mlp_copies(part)]
+    plan += [weight_copy(w.at[layer + 1], next_base + which) for which, w in enumerate((wq, wk, wv))]
     started = [0]
 
     def fetch(limit):
@@ -335,90 +379,41 @@
             copy.start()
         started[0] = max(started[0], min(limit, len(plan)))
 
+    me = lax.axis_index('ctx')
+    barrier = pltpu.get_barrier_semaphore()
+    after, before = (me + 1) % n_dev, (me + n_dev - 1) % n_dev
+    for neighbour in (after, before):
+        pl.semaphore_signal(barrier, inc=1, device_id={'ctx': neighbour}, device_id_type=MESH_ID)
     fetch(WINDOW)
-    if local_layer is not None:
-        x_send, x_halo, klt, vlt, keys, values, queries, attn_t, local_sem, halo_send, halo_recv = take(11)
-        me = lax.axis_index('ctx')
-        barrier = pltpu.get_barrier_semaphore()
-        after, before = (me + 1) % n_dev, (me + n_dev - 1) % n_dev
-        for neighbour in (after, before):
-            pl.semaphore_signal(barrier, inc=1, device_id={'ctx': neighbour}, device_id_type=MESH_ID)
-        pair = local_layer // 2
-        local_copies = [pltpu.make_async_copy(kl_ref.at[pair], klt, local_sem.at[0]), pltpu.make_async_copy(vl_ref.at[pair], vlt, local_sem.at[1])]
-        halo = pltpu.make_async_remote_copy(src_ref=x_ref if finish_layer is None else x_send, dst_ref=x_halo, send_sem=halo_send,
-                                            recv_sem=halo_recv, device_id={'ctx': after}, device_id_type=MESH_ID)
-        for copy in local_copies:
-            copy.start()
-        if finish_layer is None:
-            pl.semaphore_wait(barrier, 2)
-            halo.start()
+    pair = layer // 2
+    local_copies = [pltpu.make_async_copy(kl_ref.at[pair], klt, local_sem.at[0]), pltpu.make_async_copy(vl_ref.at[pair], vlt, local_sem.at[1])]
+    halo = pltpu.make_async_remote_copy(src_ref=x_ref, dst_ref=x_halo, send_sem=halo_send, recv_sem=halo_recv,
+                                        device_id={'ctx': after}, device_id_type=MESH_ID)
+    for copy in local_copies:
+        copy.start()
+    pl.semaphore_wait(barrier, 2)
+    halo.start()
 
     def block(at):
         fetch(at + WINDOW)
         plan[at].wait()
         return blocks[at]
 
-    def mlp(hidden, layer, base):
-        fetch(base + 3 * n_ff)
-        rows_ref[...] = rms_rows(hidden, gm_ref[layer:layer + 1, :])
-        sums[...] = hidden.astype(jnp.float32)
-
-        def activate(part):
-            gate_pre = mat(rows_ref[...], blocks[base + 3 * part])
-            up_pre = mat(rows_ref[...], blocks[base + 3 * part + 1])
-            acts[part % 2] = (jax.nn.gelu(gate_pre, approximate=True) * up_pre).astype(jnp.bfloat16)
-
-        def shrink(part):
-            sums[...] += mat(acts[part % 2], blocks[base + 3 * part + 2])
-
-        def arrive(part):
-            for copy in ff_copies(layer, base, part):
-                copy.wait()
-
-        arrive(0)
-        activate(0)
-
-        def step(part, carry):
-            arrive(part)
-            shrink(part - 1)
-            activate(part)
-            return carry
-
-        lax.fori_loop(1, n_ff, step, 0)
-        fetch(base + 3 * n_ff + WINDOW)
-        shrink(n_ff - 1)
-        return sums[...].astype(jnp.bfloat16)
-
     hidden = x_ref[...]
-    if finish_layer is not None:
-        attn = o_ref[...].T
-        hidden = (hidden.astype(jnp.float32) + mat(attn, block(0))).astype(jnp.bfloat16)
-        hidden = mlp(hidden, finish_layer, finish_base)
-    if local_layer is None:
-        y_ref[...] = hidden
-        return
-    if finish_layer is not None:
-        x_send[...] = hidden
-        pl.semaphore_wait(barrier, 2)
-        halo.start()
-
     heads, head_dim = kl_ref.shape[1], kl_ref.shape[2]
-    at = local_base - 4
-    gain = ga_ref[local_layer:local_layer + 1, :]
+    gain = ga_ref[layer:layer + 1, :]
     rows_ref[...] = rms_rows(hidden, gain)
-    key_block = block(at)
-    keys[n_rows:, :] = mat(rows_ref[...], key_block).astype(jnp.bfloat16)
-    value_block = block(at + 1)
-    values[:, n_rows:] = mat(rows_ref[...], value_block).astype(jnp.bfloat16).T
-    queries[...] = mat(rows_ref[...], block(at + 2)).astype(jnp.bfloat16).T
+    keys[n_rows:, :] = mat(rows_ref[...], block(0)).astype(jnp.bfloat16)
+    values[:, n_rows:] = mat(rows_ref[...], block(1)).astype(jnp.bfloat16).T
+    queries[...] = mat(rows_ref[...], block(2)).astype(jnp.bfloat16).T
     for copy in local_copies:
         copy.wait()
-    fetch(at + 4 + WINDOW)
+    fetch(len(plan))
     first = me == 0
     halo.wait_recv()
     rows_ref[...] = rms_rows(x_halo[...], gain)
-    keys[:n_rows, :] = jnp.where(first, klt[...].reshape(width, n_rows).T, mat(rows_ref[...], blocks[at]).astype(jnp.bfloat16))
-    values[:, :n_rows] = jnp.where(first, vlt[...].reshape(width, n_rows), mat(rows_ref[...], blocks[at + 1]).astype(jnp.bfloat16).T)
+    keys[:n_rows, :] = jnp.where(first, klt[...].reshape(width, n_rows).T, mat(rows_ref[...], blocks[0]).astype(jnp.bfloat16))
+    values[:, :n_rows] = jnp.where(first, vlt[...].reshape(width, n_rows), mat(rows_ref[...], blocks[1]).astype(jnp.bfloat16).T)
     ahead = lax.broadcasted_iota(jnp.int32, (2 * n_rows, n_rows), 0) - lax.broadcasted_iota(jnp.int32, (2 * n_rows, n_rows), 1)
     seen = (ahead > 0) & (ahead <= n_rows)
     row = lax.broadcasted_iota(jnp.int32, (2 * head_dim, n_rows), 0)
@@ -436,14 +431,18 @@
         return carry
 
     lax.fori_loop(0, heads // 2, head_pair, 0)
-    hidden = (hidden.astype(jnp.float32) + mat(attn_t[...].T, block(at + 3))).astype(jnp.bfloat16)
-    hidden = mlp(hidden, local_layer, local_base)
+    hidden = (hidden.astype(jnp.float32) + mat(attn_t[...].T, block(3))).astype(jnp.bfloat16)
+
+    def arrive(part):
+        for copy in mlp_copies(part):
+            copy.wait()
+
+    hidden = mlp_rows(hidden, gm_ref[layer:layer + 1, :], n_ff, blocks, base, arrive, rows_ref, acts, sums)
     y_ref[...] = hidden
-    rows_ref[...] = rms_rows(hidden, ga_ref[local_layer + 1:local_layer + 2, :])
-    fetch(len(plan))
+    rows_ref[...] = rms_rows(hidden, ga_ref[layer + 1:layer + 2, :])
 
     def project(which, carry):
-        weight_copy(wq.at[local_layer + 1], next_base + which).wait()
+        weight_copy(wq.at[layer + 1], next_base + which).wait()
         qkv_ref[which] = mat(rows_ref[...], blocks[next_base + which]).astype(jnp.bfloat16).T.reshape(qkv_ref.shape[1:])
         return carry
 
@@ -451,41 +450,29 @@
     halo.wait_send()
 
 
-def dense(finish_layer, local_layer, n_dev, x_rows, gains, attn_t, weights, local_t):
+def local_layer(layer, n_dev, x_rows, gains, weights, local_t):
     n_rows, width = x_rows.shape
     n_ff = weights[4].shape[2] // width
+    _, heads, head_dim, window = local_t[0].shape
     vmem = pl.BlockSpec(memory_space=pltpu.VMEM)
     hbm = pl.BlockSpec(memory_space=pl.ANY)
     bf16 = jnp.bfloat16
-    n_blocks = (0 if finish_layer is None else 1 + 3 * n_ff) + (0 if local_layer is None else 7 + 3 * n_ff)
-    args, in_specs = [x_rows, *gains], [vmem] * 3
-    out_shape, out_specs = [jax.ShapeDtypeStruct(x_rows.shape, bf16)], [vmem]
-    scratch = [pltpu.VMEM((n_blocks, width, width), bf16), pltpu.SemaphoreType.DMA((n_blocks,)),
-               pltpu.VMEM(x_rows.shape, bf16), pltpu.VMEM((2, *x_rows.shape), bf16), pltpu.VMEM(x_rows.shape, jnp.float32)]
-    if finish_layer is not None:
-        args.append(attn_t)
-        in_specs.append(vmem)
-    args += weights
-    in_specs += [hbm] * len(weights)
-    params = {}
-    if local_layer is not None:
-        args += local_t
-        in_specs += [hbm] * 2
-        _, heads, head_dim, window = local_t[0].shape
-        out_shape += [jax.ShapeDtypeStruct((3, heads, head_dim, n_rows), bf16)]
-        out_specs += [vmem]
-        scratch += [pltpu.VMEM(x_rows.shape, bf16), pltpu.VMEM(x_rows.shape, bf16),
-                    pltpu.VMEM((heads, head_dim, window), bf16), pltpu.VMEM((heads, head_dim, window), bf16),
-                    pltpu.VMEM((window + n_rows, width), bf16), pltpu.VMEM((width, window + n_rows), bf16),
-                    pltpu.VMEM((width, n_rows), bf16), pltpu.VMEM((width, n_rows), bf16),
-                    pltpu.SemaphoreType.DMA((2,)), pltpu.SemaphoreType.DMA, pltpu.SemaphoreType.DMA]
-        params = dict(collective_id=8 + local_layer, has_side_effects=True)
+    n_blocks = 7 + 3 * n_ff
     return pl.pallas_call(
-        functools.partial(dense_kernel, finish_layer, local_layer, n_dev),
-        out_shape=tuple(out_shape), in_specs=in_specs, out_specs=tuple(out_specs), scratch_shapes=scratch,
-        compiler_params=pltpu.CompilerParams(vmem_limit_bytes=60 * 2 ** 20, **params),
-        name='dense_%s_%s' % (finish_layer, local_layer),
-    )(*args)
+        functools.partial(local_kernel, layer, n_dev),
+        out_shape=(jax.ShapeDtypeStruct(x_rows.shape, bf16), jax.ShapeDtypeStruct((3, heads, head_dim, n_rows), bf16)),
+        in_specs=[vmem] * 3 + [hbm] * (len(weights) + 2), out_specs=(vmem, vmem),
+        scratch_shapes=[
+            pltpu.VMEM((n_blocks, width, width), bf16), pltpu.SemaphoreType.DMA((n_blocks,)),
+            pltpu.VMEM(x_rows.shape, bf16), pltpu.VMEM((2, *x_rows.shape), bf16), pltpu.VMEM(x_rows.shape, jnp.float32),
+            pltpu.VMEM(x_rows.shape, bf16),
+            pltpu.VMEM((heads, head_dim, window), bf16), pltpu.VMEM((heads, head_dim, window), bf16),
+            pltpu.VMEM((window + n_rows, width), bf16), pltpu.VMEM((width, window + n_rows), bf16),
+            pltpu.VMEM((width, n_rows), bf16), pltpu.VMEM((width, n_rows), bf16),
+            pltpu.SemaphoreType.DMA((2,)), pltpu.SemaphoreType.DMA, pltpu.SemaphoreType.DMA],
+        compiler_params=pltpu.CompilerParams(collective_id=8 + layer, has_side_effects=True, vmem_limit_bytes=60 * 2 ** 20),
+        name='local_%d' % layer,
+    )(x_rows, *gains, *weights, *local_t)
 
 
 def solution(mesh):
@@ -500,12 +487,10 @@
         cache_t = [by_slot(k_cache), by_slot(v_cache)]
         local_t = [by_slot(k_local), by_slot(v_local)]
         gains = [g_attn, g_mlp]
-        hidden, finish_layer, attn_t = x_rows, None, None
+        hidden = x_rows
         for pair in range(k_cache.shape[0]):
-            hidden, qkv = dense(finish_layer, 2 * pair, ctx_size, hidden, gains, attn_t, weights, local_t)
-            attn_t = global_attention(pair, ctx_size, cache_len, qkv, *cache_t)
-            attn_t = attn_t.reshape(-1, attn_t.shape[-1])
-            finish_layer = 2 * pair + 1
-        return dense(finish_layer, None, ctx_size, hidden, gains, attn_t, weights, local_t)[0]
+            hidden, qkv = local_layer(2 * pair, ctx_size, hidden, gains, weights, local_t)
+            hidden = global_layer(pair, ctx_size, cache_len, qkv, hidden, g_mlp, weights[3:], *cache_t)
+        return hidden
 
     return jax.shard_map(device_step, mesh=mesh, in_specs=in_specs, out_specs=row_spec, check_vma=False)

time: 214 us -> 209 us (0.977)
  Pallas kernels: 213 us -> 206 us
    pallas_call x5 -> x4, Pallas kernels: 213 us -> 206 us  [the longest x2 166 us: global_layer(): pl.pallas_call(functools.partial(global_kernel, n_dev // 2, pair), out_sh...]
where the time goes in v2:
time: 209 us
  Pallas kernels  206 us (99%)
    pallas_call x2, Pallas kernels, global_layer(): pl.pallas_call(functools.partial(global_kernel, n_dev // 2, pair), out_sh...  166 us
    pallas_call x2, Pallas kernels, local_layer(): pl.pallas_call(functools.partial(local_kernel, layer, n_dev), out_shape=(...  40.5 us

profile of v2, /device:TPU:113, one launch (start us, length us, event | category | flops | bytes accessed | tf_op | source)
XLA Modules:
  0.0 208.6 jit_solution(11444981087411927904)
XLA Ops:
  0.7 21.0 %local_0.1 = (bf16[256,768]{1,0:T(8,128)(2,1)}, bf16[3,12,64,256]{3,2,1,0:T(8,128)(2,1)}) custom-call(bf16[256,768]{1,0:T(8,128)(2,1)} %x_ref.1, bf16[4,768]{1,0:T(4,128)(2,1)} %ga_ref.3, bf16[4,768]{1,0:T(4,128)(2,1)} %gm_ref.7, bf16[4,768,768]{2,1,0:T(8,128)(2,1)} %wq.3, bf16[4,768,768]{2,1,0:T(8,128)(2,1)} %wk.3, bf16[4,768,768]{2,1,0:T(8,128)(2,1)} %wv.3, ...), custom_call_target="tpu_custom_call" | custom-call | tf_op jit(solution)/shard_map/local_0/pallas_call | solution.py:461
  21.7 82.8 %global_0.1.x_ref = bf16[256,768]{1,0:T(8,128)(2,1)} custom-call(s32[1]{0:T(128)S(6)} %copy.17.len_ref, bf16[3,12,64,256]{3,2,1,0:T(8,128)(2,1)} %get-tuple-element.9.qkv_ref, bf16[256,768]{1,0:T(8,128)(2,1)} %get-tuple-element.10.x_ref, bf16[4,768]{1,0:T(4,128)(2,1)} %gm_ref.7, bf16[4,768,768]{2,1,0:T(8,128)(2,1)} %wo.7, bf16[4,768,3072]{2,1,0:T(8,128)(2,1)} %wg.7, ...), custom_call_target="tpu_custom_call" | custom-call | tf_op jit(solution)/shard_map/global_0/pallas_call | solution.py:332
  104.5 19.5 %local_2.1 = (bf16[256,768]{1,0:T(8,128)(2,1)}, bf16[3,12,64,256]{3,2,1,0:T(8,128)(2,1)}) custom-call(bf16[256,768]{1,0:T(8,128)(2,1)} %global_0.1.x_ref, bf16[4,768]{1,0:T(4,128)(2,1)} %ga_ref.3, bf16[4,768]{1,0:T(4,128)(2,1)} %gm_ref.7, bf16[4,768,768]{2,1,0:T(8,128)(2,1)} %wq.3, bf16[4,768,768]{2,1,0:T(8,128)(2,1)} %wk.3, bf16[4,768,768]{2,1,0:T(8,128)(2,1)} %wv.3, ...), custom_call_target="tpu_custom_call" | custom-call | tf_op jit(solution)/shard_map/local_2/pallas_call | solution.py:461
  124.0 82.9 %global_1.1 = bf16[256,768]{1,0:T(8,128)(2,1)} custom-call(s32[1]{0:T(128)S(6)} %copy.17.len_ref, bf16[3,12,64,256]{3,2,1,0:T(8,128)(2,1)} %get-tuple-element.11.qkv_ref, bf16[256,768]{1,0:T(8,128)(2,1)} %get-tuple-element.12.x_ref, bf16[4,768]{1,0:T(4,128)(2,1)} %gm_ref.7, bf16[4,768,768]{2,1,0:T(8,128)(2,1)} %wo.7, bf16[4,768,3072]{2,1,0:T(8,128)(2,1)} %wg.7, ...), custom_call_target="tpu_custom_call" | custom-call | tf_op jit(solution)/shard_map/global_1/pallas_call | solution.py:332
  206.9 1.8 copy.18
